TPU v7x, 32 devices: a whole 2x2x4 slice. The times are simulated.
32 devices in a mesh: gx: 2 (over y), gy: 4 (over z), gz: 4 (over x, core).
Axes of the slice: x: 2, y: 2, z: 4, core: 2. Of those that a mesh axis runs over, the one named last changes fastest.
Arguments:
- positions: float32 [2, 4, 4, 3, 48], P('gx', 'gy', 'gz'), may hold values from 0 to 1
- species: int32 [2, 4, 4, 48], P('gx', 'gy', 'gz'), may hold values from 0 to 3
- neighbours: int32 [2, 4, 4, 48, 128], P('gx', 'gy', 'gz'), may hold values from 0 to 1295
- neigh_counts: int32 [2, 4, 4, 48], P('gx', 'gy', 'gz'), may hold values from 64 to 128
- embedding: bfloat16 [4, 128], replicated, may hold values from -6 to 6
- rbf_decay: float32 [16], replicated, may hold values from 0.2 to 5
- radial_weight: bfloat16 [2, 16, 128], replicated, may hold values from -1.5 to 1.5
- node_weight: bfloat16 [2, 128, 128], replicated, may hold values from -0.5 to 0.5
- readout: bfloat16 [128], replicated, may hold values from -0.5 to 0.5
- species_bias: float32 [4], replicated, may hold values from -4 to 4
Outputs:
- atom_energy: float32 [2, 4, 4, 48], P('gx', 'gy', 'gz')
- total_energy: float32 [], replicated
Inputs may be any that keep to these rules, and one draw needn't show every extreme that they name: `neighbours`: the offset code of an entry is 9 (dx + 1) + 3 (dy + 1) + (dz + 1) for a cell offset of -1, 0 or 1 along each dimension.
All inputs are finite; a program needn't handle non-finite values.
Results may differ from a plain program's by a relative error of at most 0.0028.
Values may be sent and summed in bfloat16 or wider, within the bound.
A program may use at most 64 MiB of HBM per device.

v0:
```python
import functools
import itertools
import math

import jax
import jax.numpy as jnp
from jax import lax
from jax.experimental import pallas as pl
from jax.experimental.pallas import tpu as pltpu
from jax.sharding import PartitionSpec as P

AXES = ("gx", "gy", "gz")
MESH = pl.DeviceIdType.MESH
LANES = 128
LOG2E = math.log2(math.e)


def distinct(count):
    return (0,) if count == 1 else (0, -1) if count == 2 else (0, -1, 1)


def canonical(offset, count):
    return 0 if count == 1 else -abs(offset) if count == 2 else offset


def code_of(offset):
    return 9 * (offset[0] + 1) + 3 * (offset[1] + 1) + offset[2] + 1


def fold_of(sizes, slots):
    merge = sizes[0] == 2
    lead = 18 * slots
    shift = -lead % LANES if merge else 0
    return merge, lead, shift, pl.cdiv(27 * slots + shift, LANES)


def kernel(
    sizes,
    stages,
    pos_any,
    spec_any,
    nbr_any,
    cnt_any,
    emb_any,
    decay_any,
    radial_any,
    node_any,
    readout_any,
    bias_any,
    out_ref,
    record,
    places,
    hist,
    codes,
    basis,
    feats0,
    feats1,
    *rest,
):
    anys = (
        pos_any, spec_any, nbr_any, cnt_any, emb_any, decay_any, radial_any, node_any, readout_any, bias_any,
    )
    pos_ref, spec_ref, nbr_ref, cnt_ref, emb_ref = rest[:5]
    decay_ref, radial_ref, node_ref, readout_ref, bias_ref = rest[5:10]
    load_sem = rest[10]
    loads = [
        pltpu.make_async_copy(src, dst, load_sem.at[n])
        for n, (src, dst) in enumerate(zip(anys, rest[:10]))
    ]
    rest = rest[11:]
    stage_bufs = rest[: len(stages)]
    pos_send, pos_recv, hid_send, hid_recv = rest[len(stages) : len(stages) + 4]
    stage_sems = rest[len(stages) + 4 :]
    me = tuple(lax.axis_index(name) for name in AXES)
    slots = pos_any.shape[-1]
    neighbour_count = nbr_any.shape[-1]
    features = emb_any.shape[1]
    kinds = emb_any.shape[0]
    basis_count = radial_ref.shape[1]
    layers = radial_ref.shape[0]
    tiles = basis.shape[1] // LANES
    merge, lead, shift_x, tables = fold_of(sizes, slots)
    first = (lead + shift_x) // LANES
    kept = lead if merge else 27 * slots
    hi_rows = hist.shape[0] // slots

    def device(shift):
        return tuple(
            lax.rem(coord + (delta % count), count) if delta % count else coord
            for coord, delta, count in zip(me, shift, sizes)
        )

    neighbours = [
        off for off in itertools.product(*(distinct(n) for n in sizes)) if off != (0, 0, 0)
    ]
    stage_shifts = [
        [
            shift
            for shift in itertools.product(
                *(range(n) if name in axes else (0,) for name, n in zip(AXES, sizes))
            )
            if any(shift)
        ]
        for axes in stages
    ]
    partners = {tuple((-d) % n for d, n in zip(off, sizes)) for off in neighbours}
    for shifts in stage_shifts:
        partners.update(shifts)
    barrier = pltpu.get_barrier_semaphore()
    for shift in sorted(partners):
        pl.semaphore_signal(barrier, inc=1, device_id=device(shift), device_id_type=MESH)

    for n in (0, 1, 3, 2, 4, 5, 6, 7, 8, 9):
        loads[n].start()
    for n in (0, 1, 3):
        loads[n].wait()
    record[...] = jnp.zeros(record.shape, jnp.float32)
    record[0:3, 0:slots] = pos_ref[0, 0, :, 0]
    record[3:4, 0:slots] = spec_ref[0, 0].astype(jnp.float32)
    counts = jnp.concatenate(
        [cnt_ref[0, 0].astype(jnp.float32), jnp.zeros((1, LANES - slots), jnp.float32)], axis=1
    )
    columns = jnp.transpose(
        jnp.concatenate([record[...], counts, jnp.zeros((3, LANES), jnp.float32)], axis=0)
    )[0:slots]
    own_pos = [
        jnp.broadcast_to(columns[:, c : c + 1], (slots, LANES)) for c in range(3)
    ]
    species_col = columns[:, 3:4]
    count_col = columns[:, 4:5]

    pl.semaphore_wait(barrier, len(partners))

    def place_copy(off):
        code = code_of(off)
        return pltpu.make_async_remote_copy(
            src_ref=record,
            dst_ref=places.at[code],
            send_sem=pos_send.at[code],
            recv_sem=pos_recv.at[code],
            device_id=device(tuple(-d for d in off)),
            device_id_type=MESH,
        )

    place_copies = [place_copy(off) for off in neighbours]
    for copy in place_copies:
        copy.start()

    loads[2].wait()
    raw = nbr_ref[0, 0, 0]
    live = lax.broadcasted_iota(jnp.int32, raw.shape, 1).astype(jnp.float32) < count_col
    raw = jnp.where(raw >= lead, raw + shift_x, raw)
    codes[...] = jnp.where(live, raw, hi_rows * LANES - 1)
    hi_iota = lax.broadcasted_iota(jnp.int32, (hi_rows, neighbour_count), 0)
    lo_iota = lax.broadcasted_iota(jnp.int32, (LANES, neighbour_count), 0)
    for atom in range(slots):
        row = codes[atom : atom + 1, :]
        high = jnp.where((row >> 7) == hi_iota, 1.0, 0.0).astype(jnp.bfloat16)
        low = jnp.where((row & (LANES - 1)) == lo_iota, 1.0, 0.0).astype(jnp.bfloat16)
        hist[atom * hi_rows : (atom + 1) * hi_rows, :] = lax.dot_general(
            high, low, (((1,), (1,)), ((), ())), preferred_element_type=jnp.float32
        )

    for n in range(4, 10):
        loads[n].wait()
    own_hidden = jnp.zeros((slots, features), jnp.float32)
    for kind in range(kinds):
        own_hidden = jnp.where(
            species_col == float(kind), emb_ref[kind : kind + 1, :].astype(jnp.float32), own_hidden
        )
    table_rows = feats1.shape[0]
    if table_rows > kept:
        feats1[kept:table_rows, :] = jnp.zeros((table_rows - kept, features), jnp.bfloat16)
    emb = emb_ref[...].astype(jnp.float32)
    if kinds < 8:
        emb = jnp.concatenate([emb, jnp.zeros((8 - kinds, features), jnp.float32)], axis=0)
    emb = emb.astype(jnp.bfloat16)
    scales = [decay_ref[b] * (-LOG2E) for b in range(basis_count)]

    lane = lax.broadcasted_iota(jnp.int32, (8, LANES), 1)
    sub = lax.broadcasted_iota(jnp.int32, (8, LANES), 0)
    for copy in place_copies:
        copy.wait_recv()

    flat = [jnp.zeros((4, LANES), jnp.float32) for _ in range(tables)]
    lane4 = lane[0:4]
    sub4 = sub[0:4]
    for off in itertools.product((-1, 0, 1), repeat=3):
        source = tuple(canonical(d, n) for d, n in zip(off, sizes))
        cell = record[...] if source == (0, 0, 0) else places[code_of(source)]
        for component, delta in enumerate(off):
            if delta:
                cell = jnp.where(sub4 == component, cell + float(delta), cell)
        column = code_of(off) * slots
        tile, start = divmod(column + (shift_x if column >= lead else 0), LANES)
        if start:
            cell = pltpu.roll(cell, start, 1)
        stop = start + slots
        flat[tile] = jnp.where((lane4 >= start) & (lane4 < stop), cell, flat[tile])
        if stop > LANES:
            flat[tile + 1] = jnp.where(lane4 < stop - LANES, cell, flat[tile + 1])

    for tile in range(tiles):
        span = slice(tile * LANES, (tile + 1) * LANES)
        terms = []
        for part in (tile, tile + first) if merge and tile + first < tables else (tile,):
            r2 = jnp.zeros((slots, LANES), jnp.float32)
            for c in range(3):
                delta = flat[part][c : c + 1, :] - own_pos[c]
                r2 = r2 + delta * delta
            terms.append((r2, hist[pl.ds(part, slots, stride=hi_rows), :]))
        for b in range(basis_count):
            basis[b * slots : (b + 1) * slots, span] = sum(
                jnp.exp2(r2 * scales[b]) * times for r2, times in terms
            ).astype(jnp.bfloat16)
        one_hot = jnp.where(
            flat[tile][3:4, :].astype(jnp.int32) == sub, 1.0, 0.0
        )
        feats0[span, :] = jnp.dot(
            jnp.transpose(one_hot).astype(jnp.bfloat16), emb, preferred_element_type=jnp.float32
        ).astype(jnp.bfloat16)

    def interaction(layer, feats, hidden):
        weight = radial_ref[layer].astype(jnp.float32)
        message = jnp.zeros((slots, features), jnp.float32)
        step = basis_count // 4
        for lead_b in range(0, basis_count, step):
            collected = jnp.dot(
                basis[lead_b * slots : (lead_b + step) * slots, :],
                feats[...],
                preferred_element_type=jnp.float32,
            )
            for b in range(step):
                message = message + (
                    collected[b * slots : (b + 1) * slots] * weight[lead_b + b : lead_b + b + 1]
                )
        inv_scale = lax.rsqrt(jnp.mean(message * message, axis=-1, keepdims=True) + 1e-05)
        normed = (message * inv_scale).astype(jnp.bfloat16)
        value = jnp.dot(normed, node_ref[layer], preferred_element_type=jnp.float32)
        update = value / (1.0 + jnp.exp(-value))
        return (hidden + update).astype(jnp.bfloat16)

    hidden1 = interaction(0, feats0, own_hidden)
    own_rows = pl.ds(code_of((0, 0, 0)) * slots, slots)
    feats1[own_rows, :] = hidden1

    def hidden_copy(off):
        code = code_of(off)
        return pltpu.make_async_remote_copy(
            src_ref=feats1.at[own_rows],
            dst_ref=feats1.at[pl.ds(code * slots, slots)],
            send_sem=hid_send.at[code],
            recv_sem=hid_recv.at[code],
            device_id=device(tuple(-d for d in off)),
            device_id_type=MESH,
        )

    hidden_copies = [hidden_copy(off) for off in neighbours]
    for copy in hidden_copies:
        copy.start()

    species_row = record[3:4, :]
    offsets = jnp.zeros((1, LANES), jnp.float32)
    for kind in range(kinds):
        offsets = jnp.where(species_row == float(kind), bias_ref[kind], offsets)
    offsets = jnp.where(lane[0:1] < slots, offsets, 0.0)

    for copy in hidden_copies:
        copy.wait_recv()
    for off in itertools.product((-1, 0, 1), repeat=3):
        source = tuple(canonical(d, n) for d, n in zip(off, sizes))
        if source != off and code_of(off) * slots < kept:
            feats1[pl.ds(code_of(off) * slots, slots), :] = feats1[
                pl.ds(code_of(source) * slots, slots), :
            ]
    hidden2 = interaction(1, feats1, hidden1.astype(jnp.float32))
    padded = jnp.concatenate(
        [hidden2, jnp.zeros((LANES - slots, features), jnp.bfloat16)], axis=0
    )
    readout = jnp.broadcast_to(readout_ref[...], (16, features))
    per_atom = lax.dot_general(
        readout, padded, (((1,), (1,)), ((), ())), preferred_element_type=jnp.float32
    )
    running = per_atom[0:1, :] + offsets
    out_ref[0:1, :] = running

    for axes, shifts, buf, send, recv in zip(
        stages, stage_shifts, stage_bufs, stage_sems[0::2], stage_sems[1::2]
    ):
        def rank_of(coords):
            rank = 0
            for name, coord, count in zip(AXES, coords, sizes):
                if name in axes:
                    rank = rank * count + coord
            return rank

        mine = rank_of(me)
        buf[mine] = running
        copies = []
        for index, shift in enumerate(shifts):
            copies.append(
                pltpu.make_async_remote_copy(
                    src_ref=buf.at[mine],
                    dst_ref=buf.at[mine],
                    send_sem=send.at[index],
                    recv_sem=recv.at[index],
                    device_id=device(shift),
                    device_id_type=MESH,
                )
            )
        for copy in copies:
            copy.start()
        for copy in copies:
            copy.wait_recv()
        running = jnp.sum(buf[...], axis=0)
        for copy in copies:
            copy.wait_send()
    out_ref[1:2, :] = jnp.broadcast_to(jnp.sum(running, axis=1, keepdims=True), (1, LANES))
    for copy in place_copies + hidden_copies:
        copy.wait_send()


def body(sizes, *args):
    positions, species, neighbours, _, embedding, decay, radial, _, readout, _ = args
    slots = positions.shape[-1]
    features = embedding.shape[1]
    basis_count = decay.shape[0]
    merge, lead, _, tables = fold_of(sizes, slots)
    tiles = pl.cdiv(lead if merge else 27 * slots, LANES)
    hi_rows = 16 * pl.cdiv(tables + 1, 16)
    devices = math.prod(sizes)
    stages = (AXES,) if devices <= 64 else tuple((name,) for name in AXES)
    stage_ranks = [
        math.prod(n for name, n in zip(AXES, sizes) if name in axes) for axes in stages
    ]
    vmem = pl.BlockSpec(memory_space=pltpu.VMEM)
    dma = pltpu.SemaphoreType.DMA
    scratch = [
        pltpu.VMEM((4, LANES), jnp.float32),
        pltpu.VMEM((27, 4, LANES), jnp.float32),
        pltpu.VMEM((slots * hi_rows, LANES), jnp.float32),
        pltpu.VMEM((slots, neighbours.shape[-1]), jnp.int32),
        pltpu.VMEM((basis_count * slots, tiles * LANES), jnp.bfloat16),
        pltpu.VMEM((tiles * LANES, features), jnp.bfloat16),
        pltpu.VMEM((tiles * LANES, features), jnp.bfloat16),
    ]
    scratch += [pltpu.VMEM((count, 1, LANES), jnp.float32) for count in stage_ranks]
    scratch += [dma((27,))] * 4
    for count in stage_ranks:
        scratch += [dma((max(count - 1, 1),))] * 2
    operands = (
        jnp.transpose(positions, (0, 1, 3, 2, 4)),
        *args[1:8],
        readout.reshape(1, features),
        args[9],
    )
    scratch[7:7] = [
        pltpu.SMEM(x.shape, x.dtype)
        if x.ndim == 1
        else pltpu.VMEM(x.shape, x.dtype)
        for x in operands
    ] + [dma((len(operands),))]
    out = pl.pallas_call(
        functools.partial(kernel, sizes, stages),
        out_shape=pltpu.VMEM((2, LANES), jnp.float32),
        in_specs=[pl.BlockSpec(memory_space=pl.ANY)] * len(operands),
        out_specs=vmem,
        scratch_shapes=scratch,
        compiler_params=pltpu.CompilerParams(collective_id=0, has_side_effects=True),
    )(*operands)
    return out[0, :slots].reshape(species.shape), out[1, 0]


def solution(mesh):
    sizes = tuple(mesh.shape[name] for name in AXES)
    return jax.shard_map(
        functools.partial(body, sizes),
        mesh=mesh,
        in_specs=(
            P("gx", "gy", "gz", None, None),
            P("gx", "gy", "gz", None),
            P("gx", "gy", "gz", None, None),
            P("gx", "gy", "gz", None),
            P(),
            P(),
            P(),
            P(),
            P(),
            P(),
        ),
        out_specs=(P("gx", "gy", "gz", None), P()),
        check_vma=False,
    )
```

profile of v0, /device:TPU:0, one launch (start us, length us, event | category | flops | bytes accessed | tf_op | source)
XLA Modules:
  0.0 26.1 jit_solution(2976376406578468825)
XLA Ops:
  0.6 24.4 %shard_map.113 = f32[2,128]{1,0:T(2,128)S(1)} custom-call(f32[1,1,3,1,48]{4,3,2,1,0:T(1,128)} %bitcast.5, s32[1,1,1,48]{3,2,1,0:T(1,128)} %spec_any.1, s32[1,1,1,48,128]{4,3,2,1,0:T(8,128)} %nbr_any.1, s32[1,1,1,48]{3,2,1,0:T(1,128)} %cnt_any.1, bf16[4,128]{1,0:T(4,128)(2,1)} %emb_any.1, f32[16]{0:T(128)} %decay_any.1, bf16[2,16,128]{2,1,0:T(8,128)(2,1)} %radial_any.1, ...), custom_call_target="tpu_custom_call" | custom-call | tf_op jit(solution)/shard_map/pallas_call | solution.py:363
  25.1 0.5 %slice.7 = f32[1,1]{1,0:T(1,128)} slice(f32[2,128]{1,0:T(2,128)S(1)} %shard_map.113), slice={[1:2], [0:1]} | slice | bytes 8 | tf_op jit(solution)/shard_map/slice | solution.py:371
  25.6 0.5 %slice_bitcast_fusion = f32[1,1,1,48]{3,2,1,0:T(1,128)} fusion(f32[2,128]{1,0:T(2,128)S(1)} %shard_map.113), kind=kLoop, calls=%fused_computation | loop fusion | bytes 384 | tf_op jit(solution)/shard_map/reshape;squeeze | solution.py:371
where the time goes:
time: 26.3 us; the launch traced here: 26.1 us
  Pallas kernels  24.4 us (93%)
  local copies, waits for them, and re-layouts  1.02 us (4%)
  between operations  0.64 us (2%)
    pallas_call x1, Pallas kernels, body(): pl.pallas_call(functools.partial(kernel, sizes, stages), out_shape=pltpu....  24.4 us

commit v1 on v0

v1 whole, which is shorter than its diff:
```python
import functools
import itertools
import math

import jax
import jax.numpy as jnp
from jax import lax
from jax.experimental import pallas as pl
from jax.experimental.pallas import tpu as pltpu
from jax.sharding import PartitionSpec as P

AXES = ("gx", "gy", "gz")
MESH = pl.DeviceIdType.MESH
LANES = 128
LOG2E = math.log2(math.e)


def distinct(count):
    return (0,) if count == 1 else (0, -1) if count == 2 else (0, -1, 1)


def canonical(offset, count):
    return 0 if count == 1 else -abs(offset) if count == 2 else offset


def round_up(value, unit):
    return -(-value // unit) * unit


def reach(sizes, steps):
    found = {(0, 0, 0)}
    for _ in range(steps):
        found = {
            tuple((a + b) % n for a, b, n in zip(shift, off, sizes))
            for shift in found
            for off in itertools.product((-1, 0, 1), repeat=3)
        }
    return found


def kernel(
    sizes,
    stages,
    pos_any,
    spec_any,
    nbr_any,
    cnt_any,
    emb_any,
    decay_any,
    radial_any,
    node_any,
    readout_any,
    bias_any,
    out_ref,
    places,
    cols,
    hist,
    codes,
    basis,
    feats0,
    feats1,
    *rest,
):
    anys = (
        pos_any, spec_any, nbr_any, cnt_any, emb_any, decay_any, radial_any, node_any, readout_any, bias_any,
    )
    pos_ref, spec_ref, nbr_ref, cnt_ref, emb_ref = rest[:5]
    decay_ref, radial_ref, node_ref, readout_ref, bias_ref = rest[5:10]
    local = rest[:10]
    load_sem = rest[10]
    rest = rest[11:]
    stage_bufs = rest[: len(stages)]
    pos_send, pos_recv, hid_send, hid_recv, red_send, red_recv = rest[len(stages) :]
    me = tuple(lax.axis_index(name) for name in AXES)
    slots = pos_any.shape[-1]
    neighbour_count = nbr_any.shape[-1]
    features = emb_any.shape[1]
    kinds = emb_any.shape[0]
    basis_count = radial_ref.shape[1]
    hi_rows = hist.shape[0] // slots
    block = 9 * slots
    far_base = round_up(2 * block, LANES)
    columns = basis.shape[1]
    xd, yd, zd = (distinct(n) for n in sizes)
    group = len(xd) * len(zd)
    split = len(yd) == 3

    loads = [
        pltpu.make_async_copy(src, dst, load_sem.at[n])
        for n, (src, dst) in enumerate(zip(anys, local))
    ]
    for n in (0, 1, 3, 2, 4, 5, 6, 7, 8, 9):
        loads[n].start()

    def wrapped(coord, delta, count):
        if isinstance(delta, int):
            return lax.rem(coord + (delta % count), count) if delta % count else coord
        return lax.rem(coord + delta + count, count)

    def device(shift):
        return tuple(wrapped(c, d, n) for c, d, n in zip(me, shift, sizes))

    def last_offset(coord):
        return jnp.where(2 * coord < sizes[1], -1, 1)

    side = last_offset(me[1])

    neighbours = [off for off in itertools.product(xd, yd, zd) if off != (0, 0, 0)]
    stage_shifts = [
        [
            shift
            for shift in itertools.product(
                *(range(n) if name in axes else (0,) for name, n in zip(AXES, sizes))
            )
            if any(shift)
        ]
        for axes in stages
    ]
    known = reach(sizes, 2)
    partners = {tuple((-d) % n for d, n in zip(off, sizes)) for off in neighbours}
    for shifts in stage_shifts:
        partners.update(shift for shift in shifts if shift not in known)
    barrier = pltpu.get_barrier_semaphore()
    for shift in sorted(partners):
        pl.semaphore_signal(barrier, inc=1, device_id=device(shift), device_id_type=MESH)

    def ordered_sends():
        planes = sorted(
            itertools.product(xd, zd), key=lambda o: -(abs(o[0]) + abs(o[1]))
        )
        ways = (-side, side, 0) if split else yd[::-1]
        return [
            (xo, yo, zo)
            for yo in ways
            for xo, zo in planes
            if not (isinstance(yo, int) and (xo, yo, zo) == (0, 0, 0))
        ]

    def group_of(yo):
        if isinstance(yo, int):
            return 0 if yo == 0 else 1
        return jnp.where(yo == last_offset(wrapped(me[1], -yo, sizes[1])), 2, 1)

    def sem_of(yo):
        if isinstance(yo, int):
            return 0
        return group_of(yo) - 1

    loads[0].wait()
    loads[1].wait()
    places[0] = jnp.zeros(places.shape[1:], jnp.float32)
    places[0, 0:3, 0:slots] = pos_ref[0, 0, :, 0]
    places[0, 3:4, 0:slots] = spec_ref[0, 0].astype(jnp.float32)

    def prepare():
        loads[3].wait()
        counts = jnp.concatenate(
            [cnt_ref[0, 0].astype(jnp.float32), jnp.zeros((1, LANES - slots), jnp.float32)], axis=1
        )
        turned = jnp.transpose(
            jnp.concatenate([places[0], counts, jnp.zeros((3, LANES), jnp.float32)], axis=0)
        )[0:slots]
        cols[:, 0:8] = turned
        count_col = turned[:, 4:5]
        loads[2].wait()
        raw = nbr_ref[0, 0, 0]
        live = lax.broadcasted_iota(jnp.int32, raw.shape, 1).astype(jnp.float32) < count_col
        x_step = jnp.where(raw >= 2 * block, 2, jnp.where(raw >= block, 1, 0))
        inner = raw - x_step * block
        y_low = inner < 3 * slots
        y_high = inner >= 6 * slots
        depth = inner - jnp.where(y_low, 0, jnp.where(y_high, 6 * slots, 3 * slots))
        low_base = jnp.where(side < 0, far_base, block)
        high_base = jnp.where(side < 0, block, far_base)
        place = depth + x_step * (3 * slots) + jnp.where(
            y_low, low_base, jnp.where(y_high, high_base, 0)
        )
        codes[...] = jnp.where(live, place, hi_rows * LANES - 1)
        hi_iota = lax.broadcasted_iota(jnp.int32, (hi_rows, neighbour_count), 0)
        lo_iota = lax.broadcasted_iota(jnp.int32, (LANES, neighbour_count), 0)
        for atom in range(slots):
            row = codes[atom : atom + 1, :]
            high = jnp.where((row >> 7) == hi_iota, 1.0, 0.0).astype(jnp.bfloat16)
            low = jnp.where((row & (LANES - 1)) == lo_iota, 1.0, 0.0).astype(jnp.bfloat16)
            hist[atom * hi_rows : (atom + 1) * hi_rows, :] = lax.dot_general(
                high, low, (((1,), (1,)), ((), ())), preferred_element_type=jnp.float32
            )

    early = side < 0
    pl.when(early)(prepare)
    pl.semaphore_wait(barrier, len(partners))

    def slot_of(xo, yo, zo):
        return group_of(yo) * group + xd.index(xo) * len(zd) + zd.index(zo)

    place_copies = [
        pltpu.make_async_remote_copy(
            src_ref=places.at[0],
            dst_ref=places.at[slot_of(*off)],
            send_sem=pos_send.at[0],
            recv_sem=pos_recv.at[sem_of(off[1])],
            device_id=device(tuple(-d for d in off)),
            device_id_type=MESH,
        )
        for off in ordered_sends()
    ]
    for copy in place_copies:
        copy.start()
    pl.when(jnp.logical_not(early))(prepare)

    for n in range(4, 10):
        loads[n].wait()
    near_rows = slice(2 * block, far_base)
    far_rows = slice(far_base + block, columns)
    for span in (near_rows, far_rows):
        if span.stop > span.start:
            feats1[span, :] = jnp.zeros((span.stop - span.start, features), jnp.bfloat16)
    own_pos = [jnp.broadcast_to(cols[:, c : c + 1], (slots, LANES)) for c in range(3)]
    species_col = cols[:, 3:4]
    own_hidden = jnp.zeros((slots, features), jnp.float32)
    for kind in range(kinds):
        own_hidden = jnp.where(
            species_col == float(kind), emb_ref[kind : kind + 1, :].astype(jnp.float32), own_hidden
        )
    emb = emb_ref[...].astype(jnp.float32)
    if kinds < 8:
        emb = jnp.concatenate([emb, jnp.zeros((8 - kinds, features), jnp.float32)], axis=0)
    emb = emb.astype(jnp.bfloat16)
    scales = [decay_ref[b] * (-LOG2E) for b in range(basis_count)]
    lane4 = lax.broadcasted_iota(jnp.int32, (4, LANES), 1)
    sub4 = lax.broadcasted_iota(jnp.int32, (4, LANES), 0)
    sub = lax.broadcasted_iota(jnp.int32, (8, LANES), 0)

    phases = (
        ([(0, 0), (1, -side)], 0, far_base),
        ([(2, side)], far_base, columns),
    )

    def source_slot(row, dx, dz):
        if not split:
            row = 0 if row == 0 or sizes[1] == 1 else 1
        x = xd.index(canonical(dx, sizes[0]))
        z = zd.index(canonical(dz, sizes[2]))
        return row * group + x * len(zd) + z

    def tables(phase):
        rows, first, stop = phases[phase]
        flat = [jnp.zeros((4, LANES), jnp.float32) for _ in range((stop - first) // LANES)]
        column = 0
        for row, dy in rows:
            for dx, dz in itertools.product((-1, 0, 1), repeat=2):
                cell = places[source_slot(row, dx, dz)]
                delta = jnp.zeros((4, LANES), jnp.float32)
                if dx:
                    delta = jnp.where(sub4 == 0, float(dx), delta)
                if row:
                    delta = jnp.where(sub4 == 1, jnp.asarray(dy, jnp.float32), delta)
                if dz:
                    delta = jnp.where(sub4 == 2, float(dz), delta)
                if dx or row or dz:
                    cell = cell + delta
                tile, start = divmod(column, LANES)
                if start:
                    cell = pltpu.roll(cell, start, 1)
                end = start + slots
                flat[tile] = jnp.where((lane4 >= start) & (lane4 < end), cell, flat[tile])
                if end > LANES:
                    flat[tile + 1] = jnp.where(lane4 < end - LANES, cell, flat[tile + 1])
                column += slots
        for index, table in enumerate(flat):
            span = slice(first + index * LANES, first + (index + 1) * LANES)
            r2 = jnp.zeros((slots, LANES), jnp.float32)
            for c in range(3):
                delta = table[c : c + 1, :] - own_pos[c]
                r2 = r2 + delta * delta
            times = hist[pl.ds(first // LANES + index, slots, stride=hi_rows), :]
            for b in range(basis_count):
                basis[b * slots : (b + 1) * slots, span] = (
                    jnp.exp2(r2 * scales[b]) * times
                ).astype(jnp.bfloat16)
            one_hot = jnp.where(table[3:4, :].astype(jnp.int32) == sub, 1.0, 0.0)
            feats0[span, :] = jnp.dot(
                jnp.transpose(one_hot).astype(jnp.bfloat16), emb, preferred_element_type=jnp.float32
            ).astype(jnp.bfloat16)

    def gather(layer, feats, phase, message):
        _, first, stop = phases[phase]
        weight = radial_ref[layer].astype(jnp.float32)
        step = basis_count // 4
        for lead_b in range(0, basis_count, step):
            collected = jnp.dot(
                basis[lead_b * slots : (lead_b + step) * slots, first:stop],
                feats[first:stop, :],
                preferred_element_type=jnp.float32,
            )
            for b in range(step):
                message = message + (
                    collected[b * slots : (b + 1) * slots] * weight[lead_b + b : lead_b + b + 1]
                )
        return message

    def update(layer, message, hidden):
        inv_scale = lax.rsqrt(jnp.mean(message * message, axis=-1, keepdims=True) + 1e-05)
        normed = (message * inv_scale).astype(jnp.bfloat16)
        value = jnp.dot(normed, node_ref[layer], preferred_element_type=jnp.float32)
        return (hidden + value / (1.0 + jnp.exp(-value))).astype(jnp.bfloat16)

    def landed(ref, sem):
        pltpu.make_async_copy(ref, ref, sem).wait()

    near_count = (2 if split else len(yd)) * group - 1
    far_count = group if split else 0

    message = jnp.zeros((slots, features), jnp.float32)
    if near_count:
        landed(places.at[pl.ds(0, near_count)], pos_recv.at[0])
    tables(0)
    message = gather(0, feats0, 0, message)
    if far_count:
        landed(places.at[pl.ds(0, far_count)], pos_recv.at[1])
    tables(1)
    message = gather(0, feats0, 1, message)
    hidden1 = update(0, message, own_hidden)

    def row_of(base, dx, dz):
        return base + (3 * (dx + 1) + dz + 1) * slots

    own_rows = pl.ds(row_of(0, 0, 0), slots)
    feats1[own_rows, :] = hidden1

    def target_base(yo):
        if isinstance(yo, int):
            return 0 if yo == 0 else block
        return jnp.where(group_of(yo) == 2, far_base, block)

    hidden_copies = [
        pltpu.make_async_remote_copy(
            src_ref=feats1.at[own_rows],
            dst_ref=feats1.at[pl.ds(pl.multiple_of(row_of(target_base(off[1]), off[0], off[2]), 16), slots)],
            send_sem=hid_send.at[0],
            recv_sem=hid_recv.at[sem_of(off[1])],
            device_id=device(tuple(-d for d in off)),
            device_id_type=MESH,
        )
        for off in ordered_sends()
    ]
    for copy in hidden_copies:
        copy.start()

    species_row = places[0, 3:4, :]
    offsets = jnp.zeros((1, LANES), jnp.float32)
    for kind in range(kinds):
        offsets = jnp.where(species_row == float(kind), bias_ref[kind], offsets)
    offsets = jnp.where(lane4[0:1] < slots, offsets, 0.0)

    def spread(phase):
        for row, _ in phases[phase][0]:
            base = (0, block, far_base)[row]
            from_base = (0, block, block)[row] if not split else base
            if sizes[1] == 1:
                from_base = 0
            for dx, dz in itertools.product((-1, 0, 1), repeat=2):
                source = row_of(from_base, canonical(dx, sizes[0]), canonical(dz, sizes[2]))
                if source != row_of(base, dx, dz):
                    feats1[pl.ds(row_of(base, dx, dz), slots), :] = feats1[pl.ds(source, slots), :]

    message = jnp.zeros((slots, features), jnp.float32)
    if near_count:
        landed(feats1.at[pl.ds(0, near_count * slots)], hid_recv.at[0])
    spread(0)
    message = gather(1, feats1, 0, message)
    if far_count:
        landed(feats1.at[pl.ds(0, far_count * slots)], hid_recv.at[1])
    spread(1)
    message = gather(1, feats1, 1, message)
    hidden2 = update(1, message, hidden1.astype(jnp.float32))
    padded = jnp.concatenate(
        [hidden2, jnp.zeros((LANES - slots, features), jnp.bfloat16)], axis=0
    )
    readout = jnp.broadcast_to(readout_ref[...], (16, features))
    per_atom = lax.dot_general(
        readout, padded, (((1,), (1,)), ((), ())), preferred_element_type=jnp.float32
    )
    running = per_atom[0:1, :] + offsets
    energies = running

    for index, (axes, shifts, buf) in enumerate(zip(stages, stage_shifts, stage_bufs)):
        def rank_of(coords):
            rank = 0
            for name, coord, count in zip(AXES, coords, sizes):
                if name in axes:
                    rank = rank * count + coord
            return rank

        mine = rank_of(me)
        buf[mine] = running
        copies = [
            pltpu.make_async_remote_copy(
                src_ref=buf.at[mine],
                dst_ref=buf.at[mine],
                send_sem=red_send.at[index],
                recv_sem=red_recv.at[index],
                device_id=device(shift),
                device_id_type=MESH,
            )
            for shift in sorted(
                shifts, key=lambda s: -sum(min(d, n - d) for d, n in zip(s, sizes))
            )
        ]
        for copy in copies:
            copy.start()
        if copies:
            landed(buf.at[pl.ds(0, len(copies))], red_recv.at[index])
        running = jnp.sum(buf[...], axis=0)
    out_ref[0:1, :] = energies
    out_ref[1:2, :] = jnp.broadcast_to(jnp.sum(running, axis=1, keepdims=True), (1, LANES))
    if place_copies:
        landed(places.at[pl.ds(0, len(place_copies))], pos_send.at[0])
        landed(feats1.at[pl.ds(0, len(hidden_copies) * slots)], hid_send.at[0])
    for index, (shifts, buf) in enumerate(zip(stage_shifts, stage_bufs)):
        if shifts:
            landed(buf.at[pl.ds(0, len(shifts))], red_send.at[index])


def body(sizes, *args):
    positions, species, neighbours, _, embedding, decay, radial, _, readout, _ = args
    slots = positions.shape[-1]
    features = embedding.shape[1]
    basis_count = decay.shape[0]
    columns = round_up(18 * slots, LANES) + round_up(9 * slots, LANES)
    hi_rows = 16 * pl.cdiv(columns // LANES + 1, 16)
    devices = math.prod(sizes)
    stages = (AXES,) if devices <= 64 else tuple((name,) for name in AXES)
    stage_ranks = [
        math.prod(n for name, n in zip(AXES, sizes) if name in axes) for axes in stages
    ]
    cells = math.prod(len(distinct(n)) for n in sizes)
    vmem = pl.BlockSpec(memory_space=pltpu.VMEM)
    dma = pltpu.SemaphoreType.DMA
    operands = (
        jnp.transpose(positions, (0, 1, 3, 2, 4)),
        *args[1:8],
        readout.reshape(1, features),
        args[9],
    )
    scratch = [
        pltpu.VMEM((cells, 4, LANES), jnp.float32),
        pltpu.VMEM((slots, LANES), jnp.float32),
        pltpu.VMEM((slots * hi_rows, LANES), jnp.float32),
        pltpu.VMEM((slots, neighbours.shape[-1]), jnp.int32),
        pltpu.VMEM((basis_count * slots, columns), jnp.bfloat16),
        pltpu.VMEM((columns, features), jnp.bfloat16),
        pltpu.VMEM((columns, features), jnp.bfloat16),
    ]
    scratch += [
        pltpu.SMEM(x.shape, x.dtype)
        if x.ndim == 1
        else pltpu.VMEM(x.shape, x.dtype)
        for x in operands
    ] + [dma((len(operands),))]
    scratch += [pltpu.VMEM((count, 1, LANES), jnp.float32) for count in stage_ranks]
    scratch += [dma((1,)), dma((2,)), dma((1,)), dma((2,)), dma((len(stages),)), dma((len(stages),))]
    out = pl.pallas_call(
        functools.partial(kernel, sizes, stages),
        out_shape=pltpu.VMEM((2, LANES), jnp.float32),
        in_specs=[pl.BlockSpec(memory_space=pl.ANY)] * len(operands),
        out_specs=vmem,
        scratch_shapes=scratch,
        compiler_params=pltpu.CompilerParams(collective_id=0, has_side_effects=True),
    )(*operands)
    return out[0, :slots].reshape(species.shape), out[1, 0]


def solution(mesh):
    sizes = tuple(mesh.shape[name] for name in AXES)
    return jax.shard_map(
        functools.partial(body, sizes),
        mesh=mesh,
        in_specs=(
            P("gx", "gy", "gz", None, None),
            P("gx", "gy", "gz", None),
            P("gx", "gy", "gz", None, None),
            P("gx", "gy", "gz", None),
            P(),
            P(),
            P(),
            P(),
            P(),
            P(),
        ),
        out_specs=(P("gx", "gy", "gz", None), P()),
        check_vma=False,
    )
```

time: 26.3 us -> 23.8 us (0.905)
  Pallas kernels: 24.4 us -> 22 us
    pallas_call x1, Pallas kernels: 24.4 us -> 22 us  [body(): pl.pallas_call(functools.partial(kernel, sizes, stages), out_shape=pltpu....]
where the time goes in v1:
time: 23.8 us; the launch traced here: 23.6 us
  Pallas kernels  22 us (92%)
  local copies, waits for them, and re-layouts  1.02 us (4%)
  between operations  0.64 us (3%)
    pallas_call x1, Pallas kernels, body(): pl.pallas_call(functools.partial(kernel, sizes, stages), out_shape=pltpu....  22 us
    slice x1, local copies, waits for them, and re-layouts, body(): return (out[0, :slots].reshape(species.shape), out[1, 0])  0.51 us
    another operation x1, local copies, waits for them, and re-layouts, body(): return (out[0, :slots].reshape(species.shape), out[1, 0])  0.51 us

profile of v1, /device:TPU:0, one launch (start us, length us, event | category | flops | bytes accessed | tf_op | source)
XLA Modules:
  0.0 23.6 jit_solution(13981356266410273096)
XLA Ops:
  0.6 22.0 %shard_map.113 = f32[2,128]{1,0:T(2,128)S(1)} custom-call(f32[1,1,3,1,48]{4,3,2,1,0:T(1,128)} %bitcast.5, s32[1,1,1,48]{3,2,1,0:T(1,128)} %spec_any.1, s32[1,1,1,48,128]{4,3,2,1,0:T(8,128)} %nbr_any.1, s32[1,1,1,48]{3,2,1,0:T(1,128)} %cnt_any.1, bf16[4,128]{1,0:T(4,128)(2,1)} %emb_any.1, f32[16]{0:T(128)} %decay_any.1, bf16[2,16,128]{2,1,0:T(8,128)(2,1)} %radial_any.1, ...), custom_call_target="tpu_custom_call" | custom-call | tf_op jit(solution)/shard_map/pallas_call | solution.py:463
  22.6 0.5 %slice.7 = f32[1,1]{1,0:T(1,128)} slice(f32[2,128]{1,0:T(2,128)S(1)} %shard_map.113), slice={[1:2], [0:1]} | slice | bytes 8 | tf_op jit(solution)/shard_map/slice | solution.py:471
  23.1 0.5 %slice_bitcast_fusion = f32[1,1,1,48]{3,2,1,0:T(1,128)} fusion(f32[2,128]{1,0:T(2,128)S(1)} %shard_map.113), kind=kLoop, calls=%fused_computation | loop fusion | bytes 384 | tf_op jit(solution)/shard_map/reshape;squeeze | solution.py:471

commit v2 on v1

--- a/solution.py
+++ b/solution.py
@@ -21,6 +21,14 @@
 
 def canonical(offset, count):
     return 0 if count == 1 else -abs(offset) if count == 2 else offset
+
+
+def is_set(offset):
+    return not isinstance(offset, int) or offset != 0
+
+
+def as_int(flag):
+    return int(flag) if isinstance(flag, bool) else flag.astype(jnp.int32)
 
 
 def round_up(value, unit):
@@ -70,7 +78,7 @@
     load_sem = rest[10]
     rest = rest[11:]
     stage_bufs = rest[: len(stages)]
-    pos_send, pos_recv, hid_send, hid_recv, red_send, red_recv = rest[len(stages) :]
+    pos_send, pos_recv, hid_send, hid_recv, red_send, red_recv, entered = rest[len(stages) :]
     me = tuple(lax.axis_index(name) for name in AXES)
     slots = pos_any.shape[-1]
     neighbour_count = nbr_any.shape[-1]
@@ -105,7 +113,6 @@
 
     side = last_offset(me[1])
 
-    neighbours = [off for off in itertools.product(xd, yd, zd) if off != (0, 0, 0)]
     stage_shifts = [
         [
             shift
@@ -116,25 +123,39 @@
         ]
         for axes in stages
     ]
+    def landed(ref, sem):
+        pltpu.make_async_copy(ref, ref, sem).wait()
+
+    far_z = jnp.where(lax.rem(me[2], 2) == 0, 1, -1) if len(zd) == 3 else zd[-1]
+    ways_z = (far_z, -far_z, 0) if len(zd) == 3 else zd[::-1]
+    ways_y = (-side, side) if split else yd[1:]
+
+    def target(off):
+        return tuple(wrapped(c, -d, n) for c, d, n in zip(me, off, sizes))
+
+    ring = [(xo, 0, zo) for xo in xd[::-1] for zo in ways_z if is_set(xo) or is_set(zo)]
+    across = [[(xo, yo, zo) for xo in xd[::-1] for zo in ways_z] for yo in ways_y]
+
+    def wrap_of(yo):
+        to = wrapped(me[1], -yo, sizes[1])
+        return to - me[1] > 1, me[1] - to > 1
+
     known = reach(sizes, 2)
-    partners = {tuple((-d) % n for d, n in zip(off, sizes)) for off in neighbours}
-    for shifts in stage_shifts:
-        partners.update(shift for shift in shifts if shift not in known)
+    others = sorted({s for shifts in stage_shifts for s in shifts if s not in known})
     barrier = pltpu.get_barrier_semaphore()
-    for shift in sorted(partners):
+
+    for shift in others:
         pl.semaphore_signal(barrier, inc=1, device_id=device(shift), device_id_type=MESH)
-
-    def ordered_sends():
-        planes = sorted(
-            itertools.product(xd, zd), key=lambda o: -(abs(o[0]) + abs(o[1]))
-        )
-        ways = (-side, side, 0) if split else yd[::-1]
-        return [
-            (xo, yo, zo)
-            for yo in ways
-            for xo, zo in planes
-            if not (isinstance(yo, int) and (xo, yo, zo) == (0, 0, 0))
-        ]
+    def greet(offs):
+        for off in offs:
+            pl.semaphore_signal(barrier, inc=1, device_id=target(off), device_id_type=MESH)
+
+    greet(ring)
+    greeted = len(ring) + len(others)
+    for offs in across:
+        low, high = wrap_of(offs[0][1])
+        pl.when(jnp.logical_not(high))(functools.partial(greet, offs))
+        greeted += len(offs) * (1 - as_int(low))
 
     def group_of(yo):
         if isinstance(yo, int):
@@ -142,9 +163,7 @@
         return jnp.where(yo == last_offset(wrapped(me[1], -yo, sizes[1])), 2, 1)
 
     def sem_of(yo):
-        if isinstance(yo, int):
-            return 0
-        return group_of(yo) - 1
+        return group_of(yo)
 
     loads[0].wait()
     loads[1].wait()
@@ -186,27 +205,61 @@
                 high, low, (((1,), (1,)), ((), ())), preferred_element_type=jnp.float32
             )
 
-    early = side < 0
-    pl.when(early)(prepare)
-    pl.semaphore_wait(barrier, len(partners))
-
     def slot_of(xo, yo, zo):
-        return group_of(yo) * group + xd.index(xo) * len(zd) + zd.index(zo)
-
-    place_copies = [
+        z = zd.index(zo) if isinstance(zo, int) else jnp.where(zo < 0, 1, 2)
+        return group_of(yo) * group + xd.index(xo) * len(zd) + z
+
+    def send_place(off):
         pltpu.make_async_remote_copy(
             src_ref=places.at[0],
             dst_ref=places.at[slot_of(*off)],
             send_sem=pos_send.at[0],
             recv_sem=pos_recv.at[sem_of(off[1])],
-            device_id=device(tuple(-d for d in off)),
+            device_id=target(off),
             device_id_type=MESH,
-        )
-        for off in ordered_sends()
-    ]
-    for copy in place_copies:
-        copy.start()
+        ).start()
+
+    early = side < 0
+    pl.when(early)(prepare)
+    pl.semaphore_wait(barrier, greeted)
+    for offs in across:
+        low, high = wrap_of(offs[0][1])
+
+        @pl.when(high)
+        def _():
+            pl.semaphore_signal(
+                entered, inc=1, device_id=target((0, offs[0][1], 0)), device_id_type=MESH
+            )
+
+    for off in ring:
+        send_place(off)
+    for offs in across:
+        low, high = wrap_of(offs[0][1])
+
+        @pl.when(jnp.logical_not(low))
+        def _():
+            for off in offs:
+                send_place(off)
+
     pl.when(jnp.logical_not(early))(prepare)
+
+    if group > 1:
+        landed(places.at[pl.ds(0, group - 1)], pos_recv.at[0])
+    for offs in across:
+        low, high = wrap_of(offs[0][1])
+
+        @pl.when(low)
+        def _():
+            yo = offs[0][1]
+            pl.semaphore_wait(entered, 1)
+            pltpu.make_async_remote_copy(
+                src_ref=places.at[pl.ds(0, group)],
+                dst_ref=places.at[pl.ds(group_of(yo) * group, group)],
+                send_sem=pos_send.at[0],
+                recv_sem=pos_recv.at[sem_of(yo)],
+                device_id=target((0, yo, 0)),
+                device_id_type=MESH,
+            ).start()
 
     for n in range(4, 10):
         loads[n].wait()
@@ -305,19 +358,14 @@
         value = jnp.dot(normed, node_ref[layer], preferred_element_type=jnp.float32)
         return (hidden + value / (1.0 + jnp.exp(-value))).astype(jnp.bfloat16)
 
-    def landed(ref, sem):
-        pltpu.make_async_copy(ref, ref, sem).wait()
-
-    near_count = (2 if split else len(yd)) * group - 1
-    far_count = group if split else 0
-
+    group_rows = (group - 1,) + (group,) * len(ways_y)
     message = jnp.zeros((slots, features), jnp.float32)
-    if near_count:
-        landed(places.at[pl.ds(0, near_count)], pos_recv.at[0])
+    if len(ways_y) > 0:
+        landed(places.at[pl.ds(0, group)], pos_recv.at[1])
     tables(0)
     message = gather(0, feats0, 0, message)
-    if far_count:
-        landed(places.at[pl.ds(0, far_count)], pos_recv.at[1])
+    if split:
+        landed(places.at[pl.ds(0, group)], pos_recv.at[2])
     tables(1)
     message = gather(0, feats0, 1, message)
     hidden1 = update(0, message, own_hidden)
@@ -333,19 +381,31 @@
             return 0 if yo == 0 else block
         return jnp.where(group_of(yo) == 2, far_base, block)
 
-    hidden_copies = [
-        pltpu.make_async_remote_copy(
-            src_ref=feats1.at[own_rows],
-            dst_ref=feats1.at[pl.ds(pl.multiple_of(row_of(target_base(off[1]), off[0], off[2]), 16), slots)],
-            send_sem=hid_send.at[0],
-            recv_sem=hid_recv.at[sem_of(off[1])],
-            device_id=device(tuple(-d for d in off)),
-            device_id_type=MESH,
-        )
-        for off in ordered_sends()
-    ]
-    for copy in hidden_copies:
-        copy.start()
+    def send_hidden(offs):
+        for off in offs:
+            row = row_of(target_base(off[1]), off[0], off[2])
+            pltpu.make_async_remote_copy(
+                src_ref=feats1.at[own_rows],
+                dst_ref=feats1.at[pl.ds(pl.multiple_of(row, 16), slots)],
+                send_sem=hid_send.at[0],
+                recv_sem=hid_recv.at[sem_of(off[1])],
+                device_id=target(off),
+                device_id_type=MESH,
+            ).start()
+
+    if split:
+        upper = jnp.where(me[1] == 0, 1, -1)
+        last = me[1] == sizes[1] - 1
+        to_upper = [(xo, upper, zo) for xo in xd[::-1] for zo in ways_z]
+        to_lower = [(xo, -upper, zo) for xo in xd[::-1] for zo in ways_z]
+        pl.when(jnp.logical_not(last))(functools.partial(send_hidden, to_upper))
+        send_hidden(ring)
+        send_hidden(to_lower)
+        pl.when(last)(functools.partial(send_hidden, to_upper))
+    else:
+        for offs in across + [ring]:
+            send_hidden(offs)
+    sent = len(ring) + sum(len(offs) for offs in across)
 
     species_row = places[0, 3:4, :]
     offsets = jnp.zeros((1, LANES), jnp.float32)
@@ -365,12 +425,13 @@
                     feats1[pl.ds(row_of(base, dx, dz), slots), :] = feats1[pl.ds(source, slots), :]
 
     message = jnp.zeros((slots, features), jnp.float32)
-    if near_count:
-        landed(feats1.at[pl.ds(0, near_count * slots)], hid_recv.at[0])
+    for index, count in enumerate(group_rows[:2]):
+        if count:
+            landed(feats1.at[pl.ds(0, count * slots)], hid_recv.at[index])
     spread(0)
     message = gather(1, feats1, 0, message)
-    if far_count:
-        landed(feats1.at[pl.ds(0, far_count * slots)], hid_recv.at[1])
+    if split:
+        landed(feats1.at[pl.ds(0, group * slots)], hid_recv.at[2])
     spread(1)
     message = gather(1, feats1, 1, message)
     hidden2 = update(1, message, hidden1.astype(jnp.float32))
@@ -384,6 +445,24 @@
     running = per_atom[0:1, :] + offsets
     energies = running
 
+    def ordered_shifts(axes):
+        ys = (
+            (side, *range(2, sizes[1] - 1), -side, 0) if split else tuple(range(sizes[1]))[::-1]
+        )
+        zs = (
+            (-far_z, *range(2, sizes[2] - 1), far_z, 0)
+            if len(zd) == 3
+            else tuple(range(sizes[2]))[::-1]
+        )
+        xs = tuple(range(sizes[0]))[::-1]
+        return [
+            (x, y, z)
+            for y in (ys if "gy" in axes else (0,))
+            for x in (xs if "gx" in axes else (0,))
+            for z in (zs if "gz" in axes else (0,))
+            if is_set(x) or is_set(y) or is_set(z)
+        ]
+
     for index, (axes, shifts, buf) in enumerate(zip(stages, stage_shifts, stage_bufs)):
         def rank_of(coords):
             rank = 0
@@ -403,9 +482,7 @@
                 device_id=device(shift),
                 device_id_type=MESH,
             )
-            for shift in sorted(
-                shifts, key=lambda s: -sum(min(d, n - d) for d, n in zip(s, sizes))
-            )
+            for shift in ordered_shifts(axes)
         ]
         for copy in copies:
             copy.start()
@@ -414,9 +491,9 @@
         running = jnp.sum(buf[...], axis=0)
     out_ref[0:1, :] = energies
     out_ref[1:2, :] = jnp.broadcast_to(jnp.sum(running, axis=1, keepdims=True), (1, LANES))
-    if place_copies:
-        landed(places.at[pl.ds(0, len(place_copies))], pos_send.at[0])
-        landed(feats1.at[pl.ds(0, len(hidden_copies) * slots)], hid_send.at[0])
+    if sent:
+        landed(places.at[pl.ds(0, sent)], pos_send.at[0])
+        landed(feats1.at[pl.ds(0, sent * slots)], hid_send.at[0])
     for index, (shifts, buf) in enumerate(zip(stage_shifts, stage_bufs)):
         if shifts:
             landed(buf.at[pl.ds(0, len(shifts))], red_send.at[index])
@@ -459,7 +536,8 @@
         for x in operands
     ] + [dma((len(operands),))]
     scratch += [pltpu.VMEM((count, 1, LANES), jnp.float32) for count in stage_ranks]
-    scratch += [dma((1,)), dma((2,)), dma((1,)), dma((2,)), dma((len(stages),)), dma((len(stages),))]
+    scratch += [dma((1,)), dma((3,)), dma((1,)), dma((3,)), dma((len(stages),)), dma((len(stages),))]
+    scratch += [pltpu.SemaphoreType.REGULAR]
     out = pl.pallas_call(
         functools.partial(kernel, sizes, stages),
         out_shape=pltpu.VMEM((2, LANES), jnp.float32),

time: 23.8 us -> 23.5 us (0.987)
  Pallas kernels: 22 us -> 21.7 us
    pallas_call x1, Pallas kernels: 22 us -> 21.7 us  [body(): pl.pallas_call(functools.partial(kernel, sizes, stages), out_shape=pltpu....]
where the time goes in v2:
time: 23.5 us; the launch traced here: 23.4 us
  Pallas kernels  21.7 us (92%)
  local copies, waits for them, and re-layouts  1.02 us (4%)
  between operations  0.64 us (3%)
    pallas_call x1, Pallas kernels, body(): pl.pallas_call(functools.partial(kernel, sizes, stages), out_shape=pltpu....  21.7 us
    slice x1, local copies, waits for them, and re-layouts, body(): return (out[0, :slots].reshape(species.shape), out[1, 0])  0.51 us
    another operation x1, local copies, waits for them, and re-layouts, body(): return (out[0, :slots].reshape(species.shape), out[1, 0])  0.51 us

profile of v2, /device:TPU:0, one launch (start us, length us, event | category | flops | bytes accessed | tf_op | source)
XLA Modules:
  0.0 23.4 jit_solution(13476153422977135918)
XLA Ops:
  0.6 21.7 %shard_map.113 = f32[2,128]{1,0:T(2,128)S(1)} custom-call(f32[1,1,3,1,48]{4,3,2,1,0:T(1,128)} %bitcast.5, s32[1,1,1,48]{3,2,1,0:T(1,128)} %spec_any.1, s32[1,1,1,48,128]{4,3,2,1,0:T(8,128)} %nbr_any.1, s32[1,1,1,48]{3,2,1,0:T(1,128)} %cnt_any.1, bf16[4,128]{1,0:T(4,128)(2,1)} %emb_any.1, f32[16]{0:T(128)} %decay_any.1, bf16[2,16,128]{2,1,0:T(8,128)(2,1)} %radial_any.1, ...), custom_call_target="tpu_custom_call" | custom-call | tf_op jit(solution)/shard_map/pallas_call | solution.py:541
  22.3 0.5 %slice.7 = f32[1,1]{1,0:T(1,128)} slice(f32[2,128]{1,0:T(2,128)S(1)} %shard_map.113), slice={[1:2], [0:1]} | slice | bytes 8 | tf_op jit(solution)/shard_map/slice | solution.py:549
  22.8 0.5 %slice_bitcast_fusion = f32[1,1,1,48]{3,2,1,0:T(1,128)} fusion(f32[2,128]{1,0:T(2,128)S(1)} %shard_map.113), kind=kLoop, calls=%fused_computation | loop fusion | bytes 384 | tf_op jit(solution)/shard_map/reshape;squeeze | solution.py:549

commit v3 on v2

--- a/solution.py
+++ b/solution.py
@@ -497,6 +497,17 @@
     for index, (shifts, buf) in enumerate(zip(stage_shifts, stage_bufs)):
         if shifts:
             landed(buf.at[pl.ds(0, len(shifts))], red_send.at[index])
+
+
+def finish(packed, energies, total, energies_here, total_here, sems):
+    energies_here[0, 0] = packed[0:1, 0 : energies.shape[-1]]
+    total_here[...] = packed[1:2, 0:1]
+    first = pltpu.make_async_copy(energies_here, energies, sems.at[0])
+    second = pltpu.make_async_copy(total_here, total, sems.at[1])
+    first.start()
+    second.start()
+    first.wait()
+    second.wait()
 
 
 def body(sizes, *args):
@@ -546,7 +557,22 @@
         scratch_shapes=scratch,
         compiler_params=pltpu.CompilerParams(collective_id=0, has_side_effects=True),
     )(*operands)
-    return out[0, :slots].reshape(species.shape), out[1, 0]
+    anywhere = pl.BlockSpec(memory_space=pl.ANY)
+    energies, total = pl.pallas_call(
+        finish,
+        out_shape=(
+            jax.ShapeDtypeStruct(species.shape, jnp.float32),
+            jax.ShapeDtypeStruct((1, 1), jnp.float32),
+        ),
+        in_specs=[vmem],
+        out_specs=(anywhere, anywhere),
+        scratch_shapes=[
+            pltpu.VMEM(species.shape, jnp.float32),
+            pltpu.VMEM((1, 1), jnp.float32),
+            dma((2,)),
+        ],
+    )(pltpu.with_memory_space_constraint(out, pltpu.VMEM))
+    return energies, total.reshape(())
 
 
 def solution(mesh):

time: 23.5 us -> 23 us (0.979)
  local copies, waits for them, and re-layouts: 1.02 us -> 0 us
  Pallas kernels: 21.7 us -> 22.2 us
    pallas_call x0 -> x1, Pallas kernels: none -> 0.53 us  [body(): pl.pallas_call(finish, out_shape=(jax.ShapeDtypeStruct(species.shape, jnp...]
    slice x1 -> x0, local copies, waits for them, and re-layouts: 0.51 us -> none  [body(): return (out[0, :slots].reshape(species.shape), out[1, 0])]
    another operation x1 -> x0, local copies, waits for them, and re-layouts: 0.51 us -> none  [body(): return (out[0, :slots].reshape(species.shape), out[1, 0])]
where the time goes in v3:
time: 23 us; the launch traced here: 22.9 us
  Pallas kernels  22.2 us (97%)
  between operations  0.64 us (3%)
    pallas_call x1, Pallas kernels, body(): pl.pallas_call(functools.partial(kernel, sizes, stages), out_shape=pltpu....  21.7 us
    pallas_call x1, Pallas kernels, body(): pl.pallas_call(finish, out_shape=(jax.ShapeDtypeStruct(species.shape, jnp...  0.53 us

profile of v3, /device:TPU:0, one launch (start us, length us, event | category | flops | bytes accessed | tf_op | source)
XLA Modules:
  0.0 22.9 jit_solution(3829465115363991097)
XLA Ops:
  0.6 21.7 %shard_map.113.packed = f32[2,128]{1,0:T(2,128)S(1)} custom-call(f32[1,1,3,1,48]{4,3,2,1,0:T(1,128)} %bitcast.3, s32[1,1,1,48]{3,2,1,0:T(1,128)} %spec_any.1, s32[1,1,1,48,128]{4,3,2,1,0:T(8,128)} %nbr_any.1, s32[1,1,1,48]{3,2,1,0:T(1,128)} %cnt_any.1, bf16[4,128]{1,0:T(4,128)(2,1)} %emb_any.1, f32[16]{0:T(128)} %decay_any.1, ...), custom_call_target="tpu_custom_call" | custom-call | tf_op jit(solution)/shard_map/pallas_call | solution.py:552
  22.3 0.5 %shard_map.114 = (f32[1,1,1,48]{3,2,1,0:T(1,128)}, f32[1,1]{1,0:T(1,128)}) custom-call(f32[2,128]{1,0:T(2,128)S(1)} %shard_map.113.packed), custom_call_target="tpu_custom_call" | custom-call | tf_op jit(solution)/shard_map/pallas_call | solution.py:561

commit v4 on v3

--- a/solution.py
+++ b/solution.py
@@ -136,6 +136,8 @@
     ring = [(xo, 0, zo) for xo in xd[::-1] for zo in ways_z if is_set(xo) or is_set(zo)]
     across = [[(xo, yo, zo) for xo in xd[::-1] for zo in ways_z] for yo in ways_y]
 
+    sent = len(ring) + sum(len(offs) for offs in across)
+
     def wrap_of(yo):
         to = wrapped(me[1], -yo, sizes[1])
         return to - me[1] > 1, me[1] - to > 1
@@ -158,7 +160,7 @@
         greeted += len(offs) * (1 - as_int(low))
 
     def group_of(yo):
-        if isinstance(yo, int):
+        if not is_set(yo) or not split:
             return 0 if yo == 0 else 1
         return jnp.where(yo == last_offset(wrapped(me[1], -yo, sizes[1])), 2, 1)
 
@@ -219,8 +221,6 @@
             device_id_type=MESH,
         ).start()
 
-    early = side < 0
-    pl.when(early)(prepare)
     pl.semaphore_wait(barrier, greeted)
     for offs in across:
         low, high = wrap_of(offs[0][1])
@@ -231,8 +231,12 @@
                 entered, inc=1, device_id=target((0, offs[0][1], 0)), device_id_type=MESH
             )
 
-    for off in ring:
-        send_place(off)
+    def send_ring():
+        for off in ring:
+            send_place(off)
+
+    first_plane = me[1] == 0
+    pl.when(first_plane)(send_ring)
     for offs in across:
         low, high = wrap_of(offs[0][1])
 
@@ -241,7 +245,9 @@
             for off in offs:
                 send_place(off)
 
-    pl.when(jnp.logical_not(early))(prepare)
+    pl.when(jnp.logical_not(first_plane))(send_ring)
+
+    prepare()
 
     if group > 1:
         landed(places.at[pl.ds(0, group - 1)], pos_recv.at[0])
@@ -284,9 +290,15 @@
     sub4 = lax.broadcasted_iota(jnp.int32, (4, LANES), 0)
     sub = lax.broadcasted_iota(jnp.int32, (8, LANES), 0)
 
+    plane_stop = block // LANES * LANES
+    cells = [
+        (row, dy, dx, dz, (far_base if row == 2 else row * block) + index * slots)
+        for row, dy in ((0, 0), (1, -side), (2, side))
+        for index, (dx, dz) in enumerate(itertools.product((-1, 0, 1), repeat=2))
+    ]
     phases = (
-        ([(0, 0), (1, -side)], 0, far_base),
-        ([(2, side)], far_base, columns),
+        ((0, far_base), (far_base, columns)),
+        ((0, plane_stop), (plane_stop, far_base), (far_base, columns)),
     )
 
     def source_slot(row, dx, dz):
@@ -297,29 +309,29 @@
         return row * group + x * len(zd) + z
 
     def tables(phase):
-        rows, first, stop = phases[phase]
+        first, stop = phases[0][phase]
         flat = [jnp.zeros((4, LANES), jnp.float32) for _ in range((stop - first) // LANES)]
-        column = 0
-        for row, dy in rows:
-            for dx, dz in itertools.product((-1, 0, 1), repeat=2):
-                cell = places[source_slot(row, dx, dz)]
-                delta = jnp.zeros((4, LANES), jnp.float32)
-                if dx:
-                    delta = jnp.where(sub4 == 0, float(dx), delta)
-                if row:
-                    delta = jnp.where(sub4 == 1, jnp.asarray(dy, jnp.float32), delta)
-                if dz:
-                    delta = jnp.where(sub4 == 2, float(dz), delta)
-                if dx or row or dz:
-                    cell = cell + delta
-                tile, start = divmod(column, LANES)
-                if start:
-                    cell = pltpu.roll(cell, start, 1)
-                end = start + slots
+        for row, dy, dx, dz, column in cells:
+            if column + slots <= first or column >= stop:
+                continue
+            cell = places[source_slot(row, dx, dz)]
+            delta = jnp.zeros((4, LANES), jnp.float32)
+            if dx:
+                delta = jnp.where(sub4 == 0, float(dx), delta)
+            if row:
+                delta = jnp.where(sub4 == 1, jnp.asarray(dy, jnp.float32), delta)
+            if dz:
+                delta = jnp.where(sub4 == 2, float(dz), delta)
+            if dx or row or dz:
+                cell = cell + delta
+            tile, start = divmod(column - first, LANES)
+            if start:
+                cell = pltpu.roll(cell, start, 1)
+            end = start + slots
+            if tile >= 0:
                 flat[tile] = jnp.where((lane4 >= start) & (lane4 < end), cell, flat[tile])
-                if end > LANES:
-                    flat[tile + 1] = jnp.where(lane4 < end - LANES, cell, flat[tile + 1])
-                column += slots
+            if end > LANES and tile + 1 < len(flat):
+                flat[tile + 1] = jnp.where(lane4 < end - LANES, cell, flat[tile + 1])
         for index, table in enumerate(flat):
             span = slice(first + index * LANES, first + (index + 1) * LANES)
             r2 = jnp.zeros((slots, LANES), jnp.float32)
@@ -337,7 +349,7 @@
             ).astype(jnp.bfloat16)
 
     def gather(layer, feats, phase, message):
-        _, first, stop = phases[phase]
+        first, stop = phases[layer][phase]
         weight = radial_ref[layer].astype(jnp.float32)
         step = basis_count // 4
         for lead_b in range(0, basis_count, step):
@@ -360,14 +372,11 @@
 
     group_rows = (group - 1,) + (group,) * len(ways_y)
     message = jnp.zeros((slots, features), jnp.float32)
-    if len(ways_y) > 0:
-        landed(places.at[pl.ds(0, group)], pos_recv.at[1])
-    tables(0)
-    message = gather(0, feats0, 0, message)
-    if split:
-        landed(places.at[pl.ds(0, group)], pos_recv.at[2])
-    tables(1)
-    message = gather(0, feats0, 1, message)
+    for phase in range(2):
+        if phase < len(ways_y):
+            landed(places.at[pl.ds(0, group)], pos_recv.at[phase + 1])
+        tables(phase)
+        message = gather(0, feats0, phase, message)
     hidden1 = update(0, message, own_hidden)
 
     def row_of(base, dx, dz):
@@ -377,35 +386,69 @@
     feats1[own_rows, :] = hidden1
 
     def target_base(yo):
-        if isinstance(yo, int):
+        if not is_set(yo) or not split:
             return 0 if yo == 0 else block
         return jnp.where(group_of(yo) == 2, far_base, block)
 
-    def send_hidden(offs):
+    def target_base_here(yo):
+        return jnp.where(side == yo, far_base, block)
+
+    def send_hidden(offs, out_sem, in_sem=None):
         for off in offs:
             row = row_of(target_base(off[1]), off[0], off[2])
             pltpu.make_async_remote_copy(
                 src_ref=feats1.at[own_rows],
                 dst_ref=feats1.at[pl.ds(pl.multiple_of(row, 16), slots)],
-                send_sem=hid_send.at[0],
-                recv_sem=hid_recv.at[sem_of(off[1])],
+                send_sem=hid_send.at[out_sem],
+                recv_sem=hid_recv.at[sem_of(off[1]) if in_sem is None else in_sem],
                 device_id=target(off),
                 device_id_type=MESH,
             ).start()
 
+    shared = split and len(zd) == 3 and sizes[2] % 2 == 0
+    odd = lax.rem(me[2], 2) == 1
+    last_plane = me[1] == sizes[1] - 1
+    inner_plane = jnp.logical_not(jnp.logical_or(first_plane, last_plane))
+    up = [(xo, -1, zo) for xo in xd[::-1] for zo in ways_z]
+    down = [(xo, 1, zo) for xo in xd[::-1] for zo in ways_z]
+    handed = 2 * len(xd)
+    hands_on = jnp.logical_and(odd, jnp.logical_not(first_plane))
+
+    def send_up():
+        if not shared:
+            send_hidden(up, 1)
+            return
+        send_hidden([(xo, -1, jnp.where(odd, 0, -1)) for xo in xd[::-1]], 1, 3)
+        send_hidden([(xo, -1, far_z) for xo in xd[::-1]], 1)
+
     if split:
-        upper = jnp.where(me[1] == 0, 1, -1)
-        last = me[1] == sizes[1] - 1
-        to_upper = [(xo, upper, zo) for xo in xd[::-1] for zo in ways_z]
-        to_lower = [(xo, -upper, zo) for xo in xd[::-1] for zo in ways_z]
-        pl.when(jnp.logical_not(last))(functools.partial(send_hidden, to_upper))
-        send_hidden(ring)
-        send_hidden(to_lower)
-        pl.when(last)(functools.partial(send_hidden, to_upper))
+        pl.when(first_plane)(functools.partial(send_hidden, down, 0))
+        pl.when(inner_plane)(send_up)
+        send_hidden(ring, 0)
+        pl.when(first_plane)(send_up)
+        pl.when(jnp.logical_not(first_plane))(functools.partial(send_hidden, down, 0))
+        pl.when(last_plane)(functools.partial(send_hidden, up, 1))
     else:
         for offs in across + [ring]:
-            send_hidden(offs)
-    sent = len(ring) + sum(len(offs) for offs in across)
+            send_hidden(offs, 0)
+    if shared:
+        base = target_base_here(-1)
+
+        @pl.when(hands_on)
+        def _():
+            landed(feats1.at[pl.ds(0, handed * slots)], hid_recv.at[3])
+            for xo in xd[::-1]:
+                rows = [
+                    pl.ds(pl.multiple_of(row_of(base, xo, dz), 16), 2 * slots) for dz in (-1, 0)
+                ]
+                pltpu.make_async_remote_copy(
+                    src_ref=feats1.at[rows[0]],
+                    dst_ref=feats1.at[rows[1]],
+                    send_sem=hid_send.at[2],
+                    recv_sem=hid_recv.at[jnp.where(side < 0, 2, 1)],
+                    device_id=target((0, 0, 1)),
+                    device_id_type=MESH,
+                ).start()
 
     species_row = places[0, 3:4, :]
     offsets = jnp.zeros((1, LANES), jnp.float32)
@@ -413,37 +456,33 @@
         offsets = jnp.where(species_row == float(kind), bias_ref[kind], offsets)
     offsets = jnp.where(lane4[0:1] < slots, offsets, 0.0)
 
-    def spread(phase):
-        for row, _ in phases[phase][0]:
-            base = (0, block, far_base)[row]
-            from_base = (0, block, block)[row] if not split else base
-            if sizes[1] == 1:
-                from_base = 0
-            for dx, dz in itertools.product((-1, 0, 1), repeat=2):
-                source = row_of(from_base, canonical(dx, sizes[0]), canonical(dz, sizes[2]))
-                if source != row_of(base, dx, dz):
-                    feats1[pl.ds(row_of(base, dx, dz), slots), :] = feats1[pl.ds(source, slots), :]
+    def spread(row):
+        base = (0, block, far_base)[row]
+        from_base = base if split else 0 if row == 0 or sizes[1] == 1 else block
+        for dx, dz in itertools.product((-1, 0, 1), repeat=2):
+            source = row_of(from_base, canonical(dx, sizes[0]), canonical(dz, sizes[2]))
+            if source != row_of(base, dx, dz):
+                feats1[pl.ds(row_of(base, dx, dz), slots), :] = feats1[pl.ds(source, slots), :]
 
     message = jnp.zeros((slots, features), jnp.float32)
-    for index, count in enumerate(group_rows[:2]):
-        if count:
-            landed(feats1.at[pl.ds(0, count * slots)], hid_recv.at[index])
-    spread(0)
-    message = gather(1, feats1, 0, message)
-    if split:
-        landed(feats1.at[pl.ds(0, group * slots)], hid_recv.at[2])
-    spread(1)
-    message = gather(1, feats1, 1, message)
+    for phase in range(3):
+        if phase <= len(ways_y) and group_rows[phase]:
+            whole = feats1.at[pl.ds(0, group_rows[phase] * slots)]
+            if shared and phase:
+                below = side == -1 if phase == 2 else side == 1
+                part = jnp.logical_and(hands_on, below)
+                rest_rows = feats1.at[pl.ds(0, (group_rows[phase] - handed) * slots)]
+                pl.when(part)(functools.partial(landed, rest_rows, hid_recv.at[phase]))
+                pl.when(jnp.logical_not(part))(
+                    functools.partial(landed, whole, hid_recv.at[phase])
+                )
+            else:
+                landed(whole, hid_recv.at[phase])
+        spread(phase)
+        message = gather(1, feats1, phase, message)
     hidden2 = update(1, message, hidden1.astype(jnp.float32))
-    padded = jnp.concatenate(
-        [hidden2, jnp.zeros((LANES - slots, features), jnp.bfloat16)], axis=0
-    )
-    readout = jnp.broadcast_to(readout_ref[...], (16, features))
-    per_atom = lax.dot_general(
-        readout, padded, (((1,), (1,)), ((), ())), preferred_element_type=jnp.float32
-    )
-    running = per_atom[0:1, :] + offsets
-    energies = running
+    readout_row = readout_ref[...].astype(jnp.float32)
+    running = jnp.sum(hidden2.astype(jnp.float32) * readout_row, axis=0, keepdims=True) + offsets
 
     def ordered_shifts(axes):
         ys = (
@@ -486,14 +525,37 @@
         ]
         for copy in copies:
             copy.start()
+        if index == 0:
+            padded = jnp.concatenate(
+                [hidden2, jnp.zeros((LANES - slots, features), jnp.bfloat16)], axis=0
+            )
+            per_atom = lax.dot_general(
+                jnp.broadcast_to(readout_ref[...], (16, features)),
+                padded,
+                (((1,), (1,)), ((), ())),
+                preferred_element_type=jnp.float32,
+            )
+            out_ref[0:1, :] = per_atom[0:1, :] + offsets
         if copies:
             landed(buf.at[pl.ds(0, len(copies))], red_recv.at[index])
         running = jnp.sum(buf[...], axis=0)
-    out_ref[0:1, :] = energies
     out_ref[1:2, :] = jnp.broadcast_to(jnp.sum(running, axis=1, keepdims=True), (1, LANES))
     if sent:
         landed(places.at[pl.ds(0, sent)], pos_send.at[0])
-        landed(feats1.at[pl.ds(0, sent * slots)], hid_send.at[0])
+        later = len(up) if split else 0
+        landed(feats1.at[pl.ds(0, (sent - later) * slots)], hid_send.at[0])
+    if split:
+        fewer = len(up) - handed + len(xd) if shared else len(up)
+
+        def drain(flag, count, index):
+            pl.when(flag)(
+                functools.partial(landed, feats1.at[pl.ds(0, count * slots)], hid_send.at[index])
+            )
+
+        drain(last_plane, len(up), 1)
+        drain(jnp.logical_not(last_plane), fewer, 1)
+        if shared:
+            drain(hands_on, handed, 2)
     for index, (shifts, buf) in enumerate(zip(stage_shifts, stage_bufs)):
         if shifts:
             landed(buf.at[pl.ds(0, len(shifts))], red_send.at[index])
@@ -547,7 +609,7 @@
         for x in operands
     ] + [dma((len(operands),))]
     scratch += [pltpu.VMEM((count, 1, LANES), jnp.float32) for count in stage_ranks]
-    scratch += [dma((1,)), dma((3,)), dma((1,)), dma((3,)), dma((len(stages),)), dma((len(stages),))]
+    scratch += [dma((1,)), dma((3,)), dma((3,)), dma((4,)), dma((len(stages),)), dma((len(stages),))]
     scratch += [pltpu.SemaphoreType.REGULAR]
     out = pl.pallas_call(
         functools.partial(kernel, sizes, stages),

time: 23 us -> 22.8 us (level)
  Pallas kernels: 22.2 us -> 21.9 us
    pallas_call x1, Pallas kernels: 21.7 us -> 21.4 us  [body(): pl.pallas_call(functools.partial(kernel, sizes, stages), out_shape=pltpu....]
where the time goes in v4:
time: 22.8 us; the launch traced here: 22.6 us
  Pallas kernels  21.9 us (96%)
  between operations  0.64 us (3%)
    pallas_call x1, Pallas kernels, body(): pl.pallas_call(functools.partial(kernel, sizes, stages), out_shape=pltpu....  21.4 us
    pallas_call x1, Pallas kernels, body(): pl.pallas_call(finish, out_shape=(jax.ShapeDtypeStruct(species.shape, jnp...  0.53 us

profile of v4, /device:TPU:0, one launch (start us, length us, event | category | flops | bytes accessed | tf_op | source)
XLA Modules:
  0.0 22.6 jit_solution(17925409285416652527)
XLA Ops:
  0.6 21.4 %shard_map.113.packed = f32[2,128]{1,0:T(2,128)S(1)} custom-call(f32[1,1,3,1,48]{4,3,2,1,0:T(1,128)} %bitcast.3, s32[1,1,1,48]{3,2,1,0:T(1,128)} %spec_any.1, s32[1,1,1,48,128]{4,3,2,1,0:T(8,128)} %nbr_any.1, s32[1,1,1,48]{3,2,1,0:T(1,128)} %cnt_any.1, bf16[4,128]{1,0:T(4,128)(2,1)} %emb_any.1, f32[16]{0:T(128)} %decay_any.1, ...), custom_call_target="tpu_custom_call" | custom-call | tf_op jit(solution)/shard_map/pallas_call | solution.py:614
  22.1 0.5 %shard_map.114 = (f32[1,1,1,48]{3,2,1,0:T(1,128)}, f32[1,1]{1,0:T(1,128)}) custom-call(f32[2,128]{1,0:T(2,128)S(1)} %shard_map.113.packed), custom_call_target="tpu_custom_call" | custom-call | tf_op jit(solution)/shard_map/pallas_call | solution.py:623
